TPU v7x, 32 devices: a whole 2x2x4 slice. The times are simulated.
32 devices in a mesh: gz: 8 (over z, x), gy: 4 (over y, core).
Axes of the slice: x: 2, y: 2, z: 4, core: 2. Of those that a mesh axis runs over, the one named last changes fastest.
Arguments:
- right_side: float32 [64, 32, 256], P('gz', 'gy'), may hold values from -10 to 10, as said below
Outputs:
- solution_field: float32 [64, 32, 256], P('gz', 'gy')
- residual: float32 [64, 32, 256], P('gz', 'gy')
Inputs may be any that keep to these rules, and one draw needn't show every extreme that they name: `right_side`: a right-hand side.
All inputs are finite; a program needn't handle non-finite values.
Results may differ from a plain program's by a relative error of at most 0.00015.
Values sent between devices are 32-bit elements; how exact they have to be, the bound alone decides.
A program may use at most 64 MiB of HBM per device.

v0:
```python
import jax
import jax.numpy as jnp
from jax import lax
from jax.sharding import PartitionSpec as P

LEVELS = 3


sweep_order = [
    ((0, 0), (0, 1)),
    ((0, 1), (0, 1)),
    ((1, 0), (0, 1)),
    ((1, 1), (0, 1)),
    ((1, 1), (1, 0)),
    ((1, 0), (1, 0)),
    ((0, 1), (1, 0)),
    ((0, 0), (1, 0)),
]


def extended(block, sides, width):
    for axis, dim in sides:
        count = lax.axis_size(axis)
        forward = [(i, i + 1) for i in range(count - 1)]
        backward = [(target, source) for source, target in forward]
        low = lax.ppermute(
            lax.slice_in_dim(block, block.shape[dim] - width, None, axis=dim), axis, forward
        )
        high = lax.ppermute(lax.slice_in_dim(block, 0, width, axis=dim), axis, backward)
        block = jnp.concatenate([low, block, high], axis=dim)
    return block


def x_side(field):
    width = [(0, 0)] * (field.ndim - 1)
    upper = jnp.pad(field[..., 1:], width + [(0, 1)])
    lower = jnp.pad(field[..., :-1], width + [(1, 0)])
    return upper + lower


def operate(padded):
    z_cells = padded.shape[0] - 2
    y_cells = padded.shape[1] - 2
    boxed = jnp.zeros((z_cells, y_cells, padded.shape[2]), jnp.float32)
    for z_step in range(3):
        for y_step in range(3):
            boxed = boxed + padded[z_step : z_step + z_cells, y_step : y_step + y_cells, :]
    boxed = boxed + x_side(boxed)
    return 27.0 * padded[1:-1, 1:-1, :] - boxed


def group_update(padded, rhs, z_par, y_par, x_order):
    z_cells = padded.shape[0] - 2
    y_cells = padded.shape[1] - 2
    outer = None
    for z_step in (-1, 0, 1):
        for y_step in (-1, 0, 1):
            if z_step == 0 and y_step == 0:
                continue
            row = padded[
                1 + z_par + z_step : z_cells + z_par + z_step : 2,
                1 + y_par + y_step : y_cells + y_par + y_step : 2,
                :,
            ]
            outer = row if outer is None else outer + row
    center = padded[1 + z_par : z_cells + z_par : 2, 1 + y_par : y_cells + y_par : 2, :]
    total = outer + x_side(outer) + rhs[z_par::2, y_par::2, :]
    parity = jnp.arange(padded.shape[2], dtype=jnp.int32) % 2
    for x_par in x_order:
        center = jnp.where(parity == x_par, (total + x_side(center)) / 26.0, center)
    return padded.at[1 + z_par : z_cells + z_par : 2, 1 + y_par : y_cells + y_par : 2, :].set(
        center
    )


def joint_halo(field):
    return extended(field, (("gz", 0), ("gy", 1)), 1)


def margin_depth(rhs):
    return 4 if min(rhs.shape[0], rhs.shape[1]) >= 4 else 2


def deep_border(field, depth):
    return extended(field, (("gz", 0), ("gy", 1)), depth)


def rhs_border(rhs):
    return extended(rhs, (("gz", 0), ("gy", 1)), margin_depth(rhs))


def inside_mask(rhs, depth):
    z_cells = rhs.shape[0]
    y_cells = rhs.shape[1]
    z_global = (
        lax.axis_index("gz") * z_cells - depth + jnp.arange(z_cells + 2 * depth, dtype=jnp.int32)
    )
    y_global = (
        lax.axis_index("gy") * y_cells - depth + jnp.arange(y_cells + 2 * depth, dtype=jnp.int32)
    )
    z_inside = (z_global >= 0) & (z_global < z_cells * lax.axis_size("gz"))
    y_inside = (y_global >= 0) & (y_global < y_cells * lax.axis_size("gy"))
    return (z_inside[:, None, None] & y_inside[None, :, None]).astype(jnp.float32)


def deep_sweeps(rhs, rhs_wide, start):
    depth = margin_depth(rhs)
    inner_rhs = rhs_wide[1:-1, 1:-1, :]
    inside = inside_mask(rhs, depth)
    if start is None:
        padded = jnp.zeros(rhs_wide.shape, jnp.float32)
    else:
        padded = deep_border(start, depth)
    for position in range(len(sweep_order)):
        group, x_order = sweep_order[position]
        if position > 0 and position % depth == 0:
            padded = deep_border(padded[depth:-depth, depth:-depth, :], depth)
        padded = group_update(padded, inner_rhs, 1 - group[0], 1 - group[1], x_order) * inside
    return padded[depth:-depth, depth:-depth, :]


def vcycle_deep(rhs, level):
    if level == LEVELS - 1:
        return deep_sweeps(rhs, rhs_border(rhs), None)
    rhs_wide = rhs_border(rhs)
    first = deep_sweeps(rhs, rhs_wide, None)
    defect = rhs - operate(joint_halo(first))
    coarse = vcycle_deep(defect[::2, ::2, ::2], level + 1)
    start = first.at[::2, ::2, ::2].add(coarse)
    return deep_sweeps(rhs, rhs_wide, start)


def body(right_side):
    precond = vcycle_deep(right_side, 0)
    numer = lax.psum(jnp.sum(right_side * precond), ("gz", "gy"))
    image = operate(joint_halo(precond))
    denom = lax.psum(jnp.sum(precond * image), ("gz", "gy"))
    alpha = numer / denom
    return (alpha * precond, right_side - alpha * image)


def solution(mesh):
    return jax.shard_map(
        body,
        mesh=mesh,
        in_specs=(P("gz", "gy", None),),
        out_specs=(P("gz", "gy", None), P("gz", "gy", None)),
        check_vma=False,
    )
```

profile of v0, /device:TPU:12, one launch (start us, length us, event | category | flops | bytes accessed | tf_op | source)
XLA Modules:
  0.0 494.4 jit_solution(8656599293575818760)
XLA Ops:
  18.8 3.9 scatter_fusion
  25.5 3.9 scatter_fusion.1
  31.7 3.9 scatter_fusion.2
  38.0 3.9 scatter_fusion.3
  42.0 4.4 collective-permute-start.4
  61.8 3.9 scatter_fusion.4
  67.9 3.9 scatter_fusion.5
  74.3 3.9 scatter_fusion.6
  80.8 3.9 scatter_fusion.7
  101.9 4.4 collective-permute-start.12
  113.8 4.1 collective-permute-start.15
  169.2 3.9 collective-permute-start.21
  184.9 3.9 collective-permute-start.25
  203.4 3.9 collective-permute-start.29
  222.5 3.9 collective-permute-start.33
  241.5 3.9 collective-permute-start.37
  258.0 15.2 %scatter_fusion.24 = f32[4,4,128]{2,1,0:T(4,128)S(1)} fusion(f32[4,4,128]{2,1,0:T(4,128)S(1)} %slice.2861, s32[256]{0:T(256)S(1)} %reshape.298, f32[256]{0:T(256)S(1)} %reshape.300), kind=kCustom, calls=%fused_computation.24 | custom fusion | flops 256 | bytes 6144 | tf_op jit(solution)/shard_map/scatter-add | solution.py:129
  276.0 3.9 collective-permute-start.41
  307.4 3.9 collective-permute-start.45
  335.9 14.7 %scatter_fusion.41 = f32[16384]{0:T(1024)S(1)} fusion(f32[16384]{0:T(1024)S(1)} %bitcast.39, s32[2048]{0:T(1024)S(1)} %bitcast.40, f32[2048]{0:T(1024)S(1)} %bitcast.41), kind=kCustom, calls=%fused_computation.41 | custom fusion | flops 2048 | bytes 32768
  353.5 3.9 collective-permute-start.49
  369.3 3.9 scatter_fusion.33
  375.7 3.9 scatter_fusion.34
  381.8 3.9 scatter_fusion.35
  387.9 3.9 scatter_fusion.36
  394.8 3.9 collective-permute-start.53
  410.2 3.9 scatter_fusion.37
  416.3 3.9 scatter_fusion.38
  422.7 3.9 scatter_fusion.39
  429.2 3.9 scatter_fusion.40
  436.0 3.9 collective-permute-start.57
  449.4 41.9 %all-reduce.240 = (f32[]{:T(128)}, f32[]{:T(128)}) all-reduce(f32[]{:T(128)} %get-tuple-element.3, f32[]{:T(128)} %get-tuple-element.2), channel_id=1, replica_groups=mesh['gz'=8,'gy'=4] {'gz','gy'}, use_global_device_ids=true, to_apply=%region_43.44 | all-reduce | flops 2 | bytes 16 | tf_op jit(solution)/shard_map/psum | solution.py:135
  (910 shorter events, 300.2 us)
Async XLA Ops:
  1.4 7.3 %collective-permute-start = (f32[4,8,256]{2,1,0:T(8,128)S(1)}, f32[4,8,256]{2,1,0:T(8,128)S(1)}, u32[]{:S(2)}, u32[]{:S(2)}) collective-permute-start(f32[4,8,256]{2,1,0:T(8,128)S(1)} %get-tuple-element.116), channel_id=1, source_target_pairs={{0,4},{4,8},{8,12},{12,16},{16,20},{20,24},{24,28},{1,5},{5,9},{9,... | collective-permute-start | bytes 98312 | tf_op jit(solution)/shard_map/ppermute | solution.py:26
  4.8 5.8 %collective-permute-start.1 = (f32[4,8,256]{2,1,0:T(8,128)S(1)}, f32[4,8,256]{2,1,0:T(8,128)S(1)}, u32[]{:S(2)}, u32[]{:S(2)}) collective-permute-start(f32[4,8,256]{2,1,0:T(8,128)S(1)} %get-tuple-element.115), channel_id=1, source_target_pairs={{4,0},{8,4},{12,8},{16,12},{20,16},{24,20},{28,24},{5,1},{9,5},{13... | collective-permute-start | bytes 98312 | tf_op jit(solution)/shard_map/ppermute | solution.py:29
  10.6 5.6 %collective-permute-start.2 = (f32[16,4,256]{2,1,0:T(4,128)S(1)}, f32[16,4,256]{2,1,0:T(4,128)S(1)}, u32[]{:S(2)}, u32[]{:S(2)}) collective-permute-start(f32[16,4,256]{2,1,0:T(4,128)S(1)} %get-tuple-element.97), channel_id=1, source_target_pairs={{0,1},{1,2},{2,3},{4,5},{5,6},{6,7},{8,9},{9,10},{10,11},{12,13},{... | collective-permute-start | bytes 196616 | tf_op jit(solution)/shard_map/ppermute | solution.py:26
  42.0 6.8 %collective-permute-start.4 = (f32[4,8,256]{2,1,0:T(8,128)S(1)}, f32[4,8,256]{2,1,0:T(8,128)S(1)}, u32[]{:S(2)}, u32[]{:S(2)}) collective-permute-start(f32[4,8,256]{2,1,0:T(8,128)S(1)} %get-tuple-element.89), channel_id=1, source_target_pairs={{0,4},{4,8},{8,12},{12,16},{16,20},{20,24},{24,28},{1,5},{5,9},{9,... | collective-permute-start | bytes 98312 | tf_op jit(solution)/shard_map/ppermute | solution.py:26
  46.4 5.8 %collective-permute-start.5 = (f32[4,8,256]{2,1,0:T(8,128)S(1)}, f32[4,8,256]{2,1,0:T(8,128)S(1)}, u32[]{:S(2)}, u32[]{:S(2)}) collective-permute-start(f32[4,8,256]{2,1,0:T(8,128)S(1)} %get-tuple-element.90), channel_id=1, source_target_pairs={{4,0},{8,4},{12,8},{16,12},{20,16},{24,20},{28,24},{5,1},{9,5},{13... | collective-permute-start | bytes 98312 | tf_op jit(solution)/shard_map/ppermute | solution.py:29
  52.3 5.7 %collective-permute-start.6 = (f32[16,4,256]{2,1,0:T(4,128)S(1)}, f32[16,4,256]{2,1,0:T(4,128)S(1)}, u32[]{:S(2)}, u32[]{:S(2)}) collective-permute-start(f32[16,4,256]{2,1,0:T(4,128)S(1)} %get-tuple-element.95), channel_id=1, source_target_pairs={{0,1},{1,2},{2,3},{4,5},{5,6},{6,7},{8,9},{9,10},{10,11},{12,13},{... | collective-permute-start | bytes 196616 | tf_op jit(solution)/shard_map/ppermute | solution.py:26
  84.8 6.8 %collective-permute-start.8 = (f32[1,8,256]{2,1,0:T(8,128)S(1)}, f32[1,8,256]{2,1,0:T(8,128)S(1)}, u32[]{:S(2)}, u32[]{:S(2)}) collective-permute-start(f32[1,8,256]{2,1,0:T(8,128)S(1)} %get-tuple-element.87), channel_id=1, source_target_pairs={{0,4},{4,8},{8,12},{12,16},{16,20},{20,24},{24,28},{1,5},{5,9},{9,... | collective-permute-start | bytes 24584 | tf_op jit(solution)/shard_map/ppermute | solution.py:26
  93.8 5.7 %collective-permute-start.10 = (f32[10,1,256]{2,1,0:T(1,128)S(1)}, f32[10,1,256]{2,1,0:T(1,128)S(1)}, u32[]{:S(2)}, u32[]{:S(2)}) collective-permute-start(f32[10,1,256]{2,1,0:T(1,128)S(1)} %get-tuple-element.107), channel_id=1, source_target_pairs={{0,1},{1,2},{2,3},{4,5},{5,6},{6,7},{8,9},{9,10},{10,11},{12,13},{... | collective-permute-start | bytes 30728 | tf_op jit(solution)/shard_map/ppermute | solution.py:26
  101.9 6.8 %collective-permute-start.12 = (f32[4,4,128]{2,1,0:T(4,128)S(1)}, f32[4,4,128]{2,1,0:T(4,128)S(1)}, u32[]{:S(2)}, u32[]{:S(2)}) collective-permute-start(f32[4,4,128]{2,1,0:T(4,128)S(1)} %slice.2154), channel_id=1, source_target_pairs={{0,4},{4,8},{8,12},{12,16},{16,20},{20,24},{24,28},{1,5},{5,9},{9,... | collective-permute-start | bytes 24584 | tf_op jit(solution)/shard_map/ppermute | solution.py:26
  111.8 6.4 %collective-permute-start.14 = (f32[12,4,128]{2,1,0:T(4,128)S(1)}, f32[12,4,128]{2,1,0:T(4,128)S(1)}, u32[]{:S(2)}, u32[]{:S(2)}) collective-permute-start(f32[12,4,128]{2,1,0:T(4,128)S(1)} %pad_maximum_fusion.20), channel_id=1, source_target_pairs={{0,1},{1,2},{2,3},{4,5},{5,6},{6,7},{8,9},{9,10},{10,11},{12,13},{... | collective-permute-start | bytes 73736 | tf_op jit(solution)/shard_map/ppermute | solution.py:26
  113.8 5.6 %collective-permute-start.15 = (f32[12,4,128]{2,1,0:T(4,128)S(1)}, f32[12,4,128]{2,1,0:T(4,128)S(1)}, u32[]{:S(2)}, u32[]{:S(2)}) collective-permute-start(f32[12,4,128]{2,1,0:T(4,128)S(1)} %pad_maximum_fusion.20), channel_id=1, source_target_pairs={{1,0},{2,1},{3,2},{5,4},{6,5},{7,6},{9,8},{10,9},{11,10},{13,12},{... | collective-permute-start | bytes 73736 | tf_op jit(solution)/shard_map/ppermute | solution.py:29
  134.4 6.8 %collective-permute-start.16 = (f32[4,4,128]{2,1,0:T(4,128)S(1)}, f32[4,4,128]{2,1,0:T(4,128)S(1)}, u32[]{:S(2)}, u32[]{:S(2)}) collective-permute-start(f32[4,4,128]{2,1,0:T(4,128)S(1)} %slice_multiply_fusion.2), channel_id=1, source_target_pairs={{0,4},{4,8},{8,12},{12,16},{16,20},{20,24},{24,28},{1,5},{5,9},{9,... | collective-permute-start | bytes 24584 | tf_op jit(solution)/shard_map/ppermute | solution.py:26
  143.4 5.6 %collective-permute-start.18 = (f32[12,4,128]{2,1,0:T(4,128)S(1)}, f32[12,4,128]{2,1,0:T(4,128)S(1)}, u32[]{:S(2)}, u32[]{:S(2)}) collective-permute-start(f32[12,4,128]{2,1,0:T(4,128)S(1)} %pad_maximum_fusion.21), channel_id=1, source_target_pairs={{0,1},{1,2},{2,3},{4,5},{5,6},{6,7},{8,9},{9,10},{10,11},{12,13},{... | collective-permute-start | bytes 73736 | tf_op jit(solution)/shard_map/ppermute | solution.py:26
  166.4 6.8 %collective-permute-start.20 = (f32[1,4,128]{2,1,0:T(4,128)S(1)}, f32[1,4,128]{2,1,0:T(4,128)S(1)}, u32[]{:S(2)}, u32[]{:S(2)}) collective-permute-start(f32[1,4,128]{2,1,0:T(4,128)S(1)} %get-tuple-element.99), channel_id=1, source_target_pairs={{0,4},{4,8},{8,12},{12,16},{16,20},{20,24},{24,28},{1,5},{5,9},{9,... | collective-permute-start | bytes 6152 | tf_op jit(solution)/shard_map/ppermute | solution.py:26
  174.7 5.6 %collective-permute-start.22 = (f32[6,1,128]{2,1,0:T(1,128)S(1)}, f32[6,1,128]{2,1,0:T(1,128)S(1)}, u32[]{:S(2)}, u32[]{:S(2)}) collective-permute-start(f32[6,1,128]{2,1,0:T(1,128)S(1)} %get-tuple-element.303), channel_id=1, source_target_pairs={{0,1},{1,2},{2,3},{4,5},{5,6},{6,7},{8,9},{9,10},{10,11},{12,13},{... | collective-permute-start | bytes 9224 | tf_op jit(solution)/shard_map/ppermute | solution.py:26
  182.1 6.8 %collective-permute-start.24 = (f32[2,2,64]{2,1,0:T(2,128)S(1)}, f32[2,2,64]{2,1,0:T(2,128)S(1)}, u32[]{:S(2)}, u32[]{:S(2)}) collective-permute-start(f32[2,2,64]{2,1,0:T(2,128)S(1)} %slice.2284), channel_id=1, source_target_pairs={{0,4},{4,8},{8,12},{12,16},{16,20},{20,24},{24,28},{1,5},{5,9},{9,... | collective-permute-start | bytes 3080 | tf_op jit(solution)/shard_map/ppermute | solution.py:26
  190.4 5.8 %collective-permute-start.26 = (f32[6,2,64]{2,1,0:T(2,128)S(1)}, f32[6,2,64]{2,1,0:T(2,128)S(1)}, u32[]{:S(2)}, u32[]{:S(2)}) collective-permute-start(f32[6,2,64]{2,1,0:T(2,128)S(1)} %pad_maximum_fusion.39), channel_id=1, source_target_pairs={{0,1},{1,2},{2,3},{4,5},{5,6},{6,7},{8,9},{9,10},{10,11},{12,13},{... | collective-permute-start | bytes 9224 | tf_op jit(solution)/shard_map/ppermute | solution.py:26
  200.6 6.8 %collective-permute-start.28 = (f32[2,2,64]{2,1,0:T(2,128)S(1)}, f32[2,2,64]{2,1,0:T(2,128)S(1)}, u32[]{:S(2)}, u32[]{:S(2)}) collective-permute-start(f32[2,2,64]{2,1,0:T(2,128)S(1)} %slice_multiply_fusion.6), channel_id=1, source_target_pairs={{0,4},{4,8},{8,12},{12,16},{16,20},{20,24},{24,28},{1,5},{5,9},{9,... | collective-permute-start | bytes 3080 | tf_op jit(solution)/shard_map/ppermute | solution.py:26
  208.9 6.0 %collective-permute-start.30 = (f32[6,2,64]{2,1,0:T(2,128)S(1)}, f32[6,2,64]{2,1,0:T(2,128)S(1)}, u32[]{:S(2)}, u32[]{:S(2)}) collective-permute-start(f32[6,2,64]{2,1,0:T(2,128)S(1)} %pad_maximum_fusion.40), channel_id=1, source_target_pairs={{0,1},{1,2},{2,3},{4,5},{5,6},{6,7},{8,9},{9,10},{10,11},{12,13},{... | collective-permute-start | bytes 9224 | tf_op jit(solution)/shard_map/ppermute | solution.py:26
  219.6 6.8 %collective-permute-start.32 = (f32[2,2,64]{2,1,0:T(2,128)S(1)}, f32[2,2,64]{2,1,0:T(2,128)S(1)}, u32[]{:S(2)}, u32[]{:S(2)}) collective-permute-start(f32[2,2,64]{2,1,0:T(2,128)S(1)} %slice_multiply_fusion.5), channel_id=1, source_target_pairs={{0,4},{4,8},{8,12},{12,16},{16,20},{20,24},{24,28},{1,5},{5,9},{9,... | collective-permute-start | bytes 3080 | tf_op jit(solution)/shard_map/ppermute | solution.py:26
  238.7 6.8 %collective-permute-start.36 = (f32[2,2,64]{2,1,0:T(2,128)S(1)}, f32[2,2,64]{2,1,0:T(2,128)S(1)}, u32[]{:S(2)}, u32[]{:S(2)}) collective-permute-start(f32[2,2,64]{2,1,0:T(2,128)S(1)} %slice_multiply_fusion.4), channel_id=1, source_target_pairs={{0,4},{4,8},{8,12},{12,16},{16,20},{20,24},{24,28},{1,5},{5,9},{9,... | collective-permute-start | bytes 3080 | tf_op jit(solution)/shard_map/ppermute | solution.py:26
  247.0 5.7 %collective-permute-start.38 = (f32[6,2,64]{2,1,0:T(2,128)S(1)}, f32[6,2,64]{2,1,0:T(2,128)S(1)}, u32[]{:S(2)}, u32[]{:S(2)}) collective-permute-start(f32[6,2,64]{2,1,0:T(2,128)S(1)} %pad_maximum_fusion.42), channel_id=1, source_target_pairs={{0,1},{1,2},{2,3},{4,5},{5,6},{6,7},{8,9},{9,10},{10,11},{12,13},{... | collective-permute-start | bytes 9224 | tf_op jit(solution)/shard_map/ppermute | solution.py:26
  273.2 6.8 %collective-permute-start.40 = (f32[4,4,128]{2,1,0:T(4,128)S(1)}, f32[4,4,128]{2,1,0:T(4,128)S(1)}, u32[]{:S(2)}, u32[]{:S(2)}) collective-permute-start(f32[4,4,128]{2,1,0:T(4,128)S(1)} %scatter_fusion.24), channel_id=1, source_target_pairs={{0,4},{4,8},{8,12},{12,16},{16,20},{20,24},{24,28},{1,5},{5,9},{9,... | collective-permute-start | bytes 24584 | tf_op jit(solution)/shard_map/ppermute | solution.py:26
  281.5 6.5 %collective-permute-start.42 = (f32[12,4,128]{2,1,0:T(4,128)S(1)}, f32[12,4,128]{2,1,0:T(4,128)S(1)}, u32[]{:S(2)}, u32[]{:S(2)}) collective-permute-start(f32[12,4,128]{2,1,0:T(4,128)S(1)} %constant_dynamic-update-slice_fusion.3), channel_id=1, source_target_pairs={{0,1},{1,2},{2,3},{4,5},{5,6},{6,7},{8,9},{9,10},{10,11},{12,13},{... | collective-permute-start | bytes 73736 | tf_op jit(solution)/shard_map/ppermute | solution.py:26
  304.5 6.8 %collective-permute-start.44 = (f32[4,4,128]{2,1,0:T(4,128)S(1)}, f32[4,4,128]{2,1,0:T(4,128)S(1)}, u32[]{:S(2)}, u32[]{:S(2)}) collective-permute-start(f32[4,4,128]{2,1,0:T(4,128)S(1)} %slice_multiply_fusion.1), channel_id=1, source_target_pairs={{0,4},{4,8},{8,12},{12,16},{16,20},{20,24},{24,28},{1,5},{5,9},{9,... | collective-permute-start | bytes 24584 | tf_op jit(solution)/shard_map/ppermute | solution.py:26
  312.9 5.8 %collective-permute-start.46 = (f32[12,4,128]{2,1,0:T(4,128)S(1)}, f32[12,4,128]{2,1,0:T(4,128)S(1)}, u32[]{:S(2)}, u32[]{:S(2)}) collective-permute-start(f32[12,4,128]{2,1,0:T(4,128)S(1)} %pad_maximum_fusion.26), channel_id=1, source_target_pairs={{0,1},{1,2},{2,3},{4,5},{5,6},{6,7},{8,9},{9,10},{10,11},{12,13},{... | collective-permute-start | bytes 73736 | tf_op jit(solution)/shard_map/ppermute | solution.py:26
  350.7 6.8 %collective-permute-start.48 = (f32[4,8,256]{2,1,0:T(8,128)S(1)}, f32[4,8,256]{2,1,0:T(8,128)S(1)}, u32[]{:S(2)}, u32[]{:S(2)}) collective-permute-start(f32[4,8,256]{2,1,0:T(8,128)S(1)} %reshape.152), channel_id=1, source_target_pairs={{0,4},{4,8},{8,12},{12,16},{16,20},{20,24},{24,28},{1,5},{5,9},{9,... | collective-permute-start | bytes 98312 | tf_op jit(solution)/shard_map/ppermute | solution.py:26
  353.5 5.8 %collective-permute-start.49 = (f32[4,8,256]{2,1,0:T(8,128)S(1)}, f32[4,8,256]{2,1,0:T(8,128)S(1)}, u32[]{:S(2)}, u32[]{:S(2)}) collective-permute-start(f32[4,8,256]{2,1,0:T(8,128)S(1)} %reshape.153), channel_id=1, source_target_pairs={{4,0},{8,4},{12,8},{16,12},{20,16},{24,20},{28,24},{5,1},{9,5},{13... | collective-permute-start | bytes 98312 | tf_op jit(solution)/shard_map/ppermute | solution.py:29
  392.0 6.8 %collective-permute-start.52 = (f32[4,8,256]{2,1,0:T(8,128)S(1)}, f32[4,8,256]{2,1,0:T(8,128)S(1)}, u32[]{:S(2)}, u32[]{:S(2)}) collective-permute-start(f32[4,8,256]{2,1,0:T(8,128)S(1)} %get-tuple-element.83), channel_id=1, source_target_pairs={{0,4},{4,8},{8,12},{12,16},{16,20},{20,24},{24,28},{1,5},{5,9},{9,... | collective-permute-start | bytes 98312 | tf_op jit(solution)/shard_map/ppermute | solution.py:26
  394.8 5.8 %collective-permute-start.53 = (f32[4,8,256]{2,1,0:T(8,128)S(1)}, f32[4,8,256]{2,1,0:T(8,128)S(1)}, u32[]{:S(2)}, u32[]{:S(2)}) collective-permute-start(f32[4,8,256]{2,1,0:T(8,128)S(1)} %get-tuple-element.84), channel_id=1, source_target_pairs={{4,0},{8,4},{12,8},{16,12},{20,16},{24,20},{28,24},{5,1},{9,5},{13... | collective-permute-start | bytes 98312 | tf_op jit(solution)/shard_map/ppermute | solution.py:29
  400.6 5.8 %collective-permute-start.54 = (f32[16,4,256]{2,1,0:T(4,128)S(1)}, f32[16,4,256]{2,1,0:T(4,128)S(1)}, u32[]{:S(2)}, u32[]{:S(2)}) collective-permute-start(f32[16,4,256]{2,1,0:T(4,128)S(1)} %get-tuple-element.91), channel_id=1, source_target_pairs={{0,1},{1,2},{2,3},{4,5},{5,6},{6,7},{8,9},{9,10},{10,11},{12,13},{... | collective-permute-start | bytes 196616 | tf_op jit(solution)/shard_map/ppermute | solution.py:26
  433.2 6.8 %collective-permute-start.56 = (f32[1,8,256]{2,1,0:T(8,128)S(1)}, f32[1,8,256]{2,1,0:T(8,128)S(1)}, u32[]{:S(2)}, u32[]{:S(2)}) collective-permute-start(f32[1,8,256]{2,1,0:T(8,128)S(1)} %get-tuple-element.81), channel_id=1, source_target_pairs={{0,4},{4,8},{8,12},{12,16},{16,20},{20,24},{24,28},{1,5},{5,9},{9,... | collective-permute-start | bytes 24584 | tf_op jit(solution)/shard_map/ppermute | solution.py:26
  (31 other events, 158.2 us)
where the time goes:
time: 504 us; the launch traced here: 494 us
  starting transfers between devices  186 us (37%)
  local copies, waits for them, and re-layouts  166 us (33%)
  waiting for transfers between devices  48.2 us (10%)
  other arithmetic  45.2 us (9%)
  blocking collectives  41.9 us (8%)
  between operations  7.55 us (1%)
    ppermute x30, starting transfers between devices, extended(): lax.ppermute(lax.slice_in_dim(block, 0, width, axis=dim), axis, backward)  110 us
    scatter x40, local copies, waits for them, and re-layouts, group_update(): padded.at[1 + z_par:z_cells + z_par:2, 1 + y_par:y_cells + y_par:2, :]  103 us
    ppermute x30, starting transfers between devices, extended(): lax.ppermute(lax.slice_in_dim(block, block.shape[dim] - width, None, axis...  75.8 us
    ppermute x30, waiting for transfers between devices, extended(): lax.ppermute(lax.slice_in_dim(block, 0, width, axis=dim), axis, backward)  48.1 us
    slice x296, local copies, waits for them, and re-layouts, group_update(): padded[1 + z_par + z_step:z_cells + z_par + z_step:2, 1 + y_par + y_step:...  42.2 us
    psum x1, blocking collectives, body(): numer = lax.psum(jnp.sum(right_side * precond), ('gz', 'gy'))  41.9 us
    scatter-add x1, other arithmetic, vcycle_deep(): start = first.at[::2, ::2, ::2].add(coarse)  15.2 us
    unnamed x4, other arithmetic  14.9 us
  transfers between devices with their start and end apart: 60, of which 30 were waited for; matrix products, arithmetic and copies ran while one was open for 0% of the time, Pallas kernels for 0%

commit v1 on v0

v1 whole, which is shorter than its diff:
```python
import functools

import jax
import jax.numpy as jnp
from jax import lax
from jax.experimental import pallas as pl
from jax.experimental.pallas import tpu as pltpu
from jax.sharding import PartitionSpec as P

MESH = pl.DeviceIdType.MESH
F32 = jnp.float32

LOW0, LOW1, LOW2 = 4, 6, 2
EVENS, ODDS = 9, 8
WINDOW = EVENS + ODDS

PHASE_A = ((0, (0, 1)), (1, (0, 1)))
PHASE_B = ((0, (0, 1)), (1, (0, 1, 0)), (0, (1, 0)))
PHASE_C = ((1, (1, 0)), (0, (1, 0)))

CHUNK0 = 3
CHUNK1 = 9


def add(*terms):
    total = None
    for term in terms:
        if term is not None:
            total = term if total is None else total + term
    return total


def shift(x, axis, step):
    if x is None:
        return None
    size = x.shape[axis]
    moved = pltpu.roll(x, step % size, axis)
    index = lax.broadcasted_iota(jnp.int32, x.shape, axis)
    keep = index >= step if step > 0 else index < size + step
    return jnp.where(keep, moved, 0.0)


def pair_sum(other, parity, axis):
    return add(other, shift(other, axis, 1 if parity == 0 else -1))


def both_sides(x, axis, step):
    return add(shift(x, axis, step), shift(x, axis, -step))


def scale_rows(shape, first, count):
    row = first + 2 * lax.broadcasted_iota(jnp.int32, shape, 0)
    return jnp.where((row >= 0) & (row < count), F32(1.0 / 26.0), F32(0.0))


def box0(s):
    tall = [[add(s[yp][xp], pair_sum(s[1 - yp][xp], yp, 1)) for xp in (0, 1)] for yp in (0, 1)]
    return [[add(tall[yp][xp], pair_sum(tall[yp][1 - xp], xp, 2)) for xp in (0, 1)] for yp in (0, 1)]


def phase0(v, g, scale, steps):
    v = [list(v[0]), list(v[1])]
    for yp, order in steps:
        w = [pair_sum(v[1 - yp][xp], yp, 1) for xp in (0, 1)]
        for xp in order:
            side = pair_sum(add(w[1 - xp], v[yp][1 - xp]), xp, 2)
            v[yp][xp] = add(g[yp][xp], w[xp], side) * scale
    return v


def box1(s):
    tall = [add(s[yp], pair_sum(s[1 - yp], yp, 1)) for yp in (0, 1)]
    return [add(t, both_sides(t, 2, 1)) for t in tall]


def phase1(v, g, scale, steps):
    v = list(v)
    shape = scale.shape
    parity = lax.broadcasted_iota(jnp.int32, shape, 2) % 2
    for yp, order in steps:
        w = pair_sum(v[1 - yp], yp, 1)
        for xp in order:
            new = add(g[yp], w, both_sides(add(w, v[yp]), 2, 1)) * scale
            v[yp] = jnp.where(parity == xp, new, 0.0 if v[yp] is None else v[yp])
    return v


def box2(s):
    if s is None:
        return None
    tall = add(s, both_sides(s, 1, 1))
    return add(tall, both_sides(tall, 2, 2))


def phase2(v, g, scale, steps):
    shape = scale.shape
    y_par = lax.broadcasted_iota(jnp.int32, shape, 1) % 2
    x_par = (lax.broadcasted_iota(jnp.int32, shape, 2) // 2) % 2
    for yp, order in steps:
        w = both_sides(v, 1, 1)
        for xp in order:
            new = add(g, w, both_sides(add(w, v), 2, 2)) * scale
            v = jnp.where((y_par == yp) & (x_par == xp), new, 0.0 if v is None else v)
    return v


def chunks(low, high, size):
    for start in range(low, high, size):
        yield start, min(size, high - start)


YX = [(0, 0), (0, 1), (1, 0), (1, 1)]


def run0(v, f, z0, z_count, odd, low, high, steps, fresh):
    for at, n in chunks(low, high, CHUNK0):
        here = pl.ds(at, n)
        below, above = (pl.ds(at, n), pl.ds(at + 1, n)) if odd else (pl.ds(at - 1, n), pl.ds(at, n))
        rhs = [[f[odd][yp, xp, here] for xp in (0, 1)] for yp in (0, 1)]
        shape = rhs[0][0].shape
        scale = scale_rows(shape, z0 + 2 * at - LOW0 + odd, z_count)
        g = rhs
        if fresh > 0:
            s = [[v[1 - odd][yp, xp, below] + v[1 - odd][yp, xp, above] for xp in (0, 1)] for yp in (0, 1)]
            b = box0(s)
            g = [[rhs[yp][xp] + b[yp][xp] for xp in (0, 1)] for yp in (0, 1)]
        old = [[v[odd][yp, xp, here] if fresh > 1 else None for xp in (0, 1)] for yp in (0, 1)]
        new = phase0(old, g, scale, steps)
        for yp, xp in YX:
            v[odd][yp, xp, here] = new[yp][xp]


def run1(v, f, z0, z_count, odd, low, high, steps, fresh):
    for at, n in chunks(low, high, CHUNK1):
        here = pl.ds(at, n)
        below, above = (pl.ds(at, n), pl.ds(at + 1, n)) if odd else (pl.ds(at - 1, n), pl.ds(at, n))
        g = [f[odd, yp, here] for yp in (0, 1)]
        scale = scale_rows(g[0].shape, z0 + 2 * at - LOW1 + odd, z_count)
        if fresh > 0:
            b = box1([v[1 - odd][yp, below] + v[1 - odd][yp, above] for yp in (0, 1)])
            g = [g[yp] + b[yp] for yp in (0, 1)]
        old = [v[odd][yp, here] if fresh > 1 else None for yp in (0, 1)]
        new = phase1(old, g, scale, steps)
        for yp in (0, 1):
            v[odd][yp, here] = new[yp]


def permutation(size, inverse):
    half = size // 2
    wide = lax.broadcasted_iota(jnp.int32, (size, size), 0 if inverse else 1)
    tall = lax.broadcasted_iota(jnp.int32, (size, size), 1 if inverse else 0)
    source = jnp.where(wide < half, 2 * wide, 2 * (wide - half) + 1)
    return jnp.where(tall == source, F32(1.0), F32(0.0))


def kernel(
    gz_n, gy_n, rhs_ref, sol_ref, res_ref,
    flat, mine, got, fe, fo, ve, vo, dbuf, cmine, cgot, f1, v1e, v1o, vc, part, parts, nat,
    s1, r1, s2, r2, s3, r3,
):
    gz, gy = lax.axis_index("gz"), lax.axis_index("gy")
    zl, yl, nx = rhs_ref.shape
    y2, x2 = yl // 2, nx // 2
    yc = y2 // 2
    zc = zl // 2
    z_count = gz_n * zl
    z0 = gz * zl
    f, v = (fe, fo), (ve, vo)
    v1 = (v1e, v1o)

    def there(dz):
        return (gz + dz >= 0) & (gz + dz < gz_n)

    split = jnp.dot(
        rhs_ref[...].reshape(zl * yl, nx), permutation(nx, False),
        precision=lax.Precision.HIGHEST, preferred_element_type=F32,
    )
    for xp in (0, 1):
        flat[xp] = split[:, xp * x2 : (xp + 1) * x2]
    for z in range(zl):
        for yp, xp in YX:
            row = flat[xp, pl.ds(z * yl + yp, y2, stride=2), :]
            mine[z, (yp * 2 + xp) * y2 : (yp * 2 + xp + 1) * y2, :] = row
    got[gy, pl.ds(LOW0, zl)] = mine[...]

    @pl.when(gz == 0)
    def _():
        got[:, 0:LOW0] = jnp.zeros((gy_n, LOW0) + got.shape[2:], F32)

    @pl.when(gz == gz_n - 1)
    def _():
        got[:, LOW0 + zl :] = jnp.zeros((gy_n, WINDOW - LOW0 - zl) + got.shape[2:], F32)

    high = WINDOW - LOW0 - zl
    moves1 = {-1: (0, high, LOW0 + zl), 0: (0, zl, LOW0), 1: (zl - LOW0, LOW0, 0)}
    moves2 = {
        -2: (0, zc // 2, 7), -1: (0, zc // 2, 5), 0: (0, zc // 2, 3), 1: (0, zc // 2, 1), 2: (zc // 2 - 1, 1, 0),
    }

    def exchange(moves, source, target, ssem, rsem):
        sends, receives = [], []
        for slot, (dz, (first, n, to)) in enumerate(moves.items()):
            for dg in range(gy_n):
                if dz == 0 and dg == 0:
                    continue
                g = lax.rem(gy + dg, gy_n)
                send = pltpu.make_async_remote_copy(
                    src_ref=source.at[pl.ds(first, n)],
                    dst_ref=target.at[gy, pl.ds(to, n)],
                    send_sem=ssem.at[slot, dg],
                    recv_sem=rsem.at[slot, gy],
                    device_id=(gz + dz, g),
                    device_id_type=MESH,
                )
                receive = pltpu.make_async_remote_copy(
                    src_ref=source.at[pl.ds(first, n)],
                    dst_ref=target.at[g, pl.ds(to, n)],
                    send_sem=ssem.at[slot, dg],
                    recv_sem=rsem.at[slot, g],
                    device_id=(gz + dz, g),
                    device_id_type=MESH,
                )
                sends.append((dz, send))
                receives.append((-dz, receive))

        def each(items, act):
            for dz in sorted(moves, key=lambda d: -abs(d)):
                group = [item for at, item in items if at == dz]

                def go(group=group):
                    for item in group:
                        act(item)

                if dz == 0:
                    go()
                else:
                    pl.when(there(dz))(go)

        each(sends, lambda c: c.start())
        return lambda: (each(receives, lambda c: c.wait_recv()), each(sends, lambda c: c.wait_send()))

    exchange(moves1, mine, got, s1, r1)()

    for q in range(WINDOW):
        for k, (yp, xp) in enumerate(YX):
            for g in range(gy_n):
                f[q % 2][yp, xp, q // 2, g * y2 : (g + 1) * y2, :] = got[g, q, k * y2 : (k + 1) * y2, :]

    run0(v, f, z0, z_count, 0, 0, EVENS, PHASE_A, 0)
    run0(v, f, z0, z_count, 1, 0, ODDS, PHASE_B, 1)
    run0(v, f, z0, z_count, 0, 1, EVENS - 1, PHASE_C, 2)

    own = LOW0 // 2
    here, below, above = pl.ds(own, zc), pl.ds(own - 1, zc), pl.ds(own, zc)
    s = [[ve[yp, xp, here] + vo[yp, xp, below] + vo[yp, xp, above] for xp in (0, 1)] for yp in (0, 1)]
    tall = [s[0][xp] + pair_sum(s[1][xp], 0, 1) for xp in (0, 1)]
    dbuf[...] = fe[0, 0, here] - (27.0 * ve[0, 0, here] - (tall[0] + pair_sum(tall[1], 0, 2)))
    for z in range(zc):
        for yp in (0, 1):
            at = ((z % 2) * 2 + yp) * yc
            cmine[z // 2, at : at + yc, :] = dbuf[z, pl.ds(gy * y2 + yp, yc, stride=2), :]
    cgot[gy, pl.ds(3, zc // 2)] = cmine[...]
    for edge, low, n in ((0, 0, 3), (1, 0, 1), (gz_n - 2, 7, 2), (gz_n - 1, 5, 4)):

        @pl.when(gz == edge)
        def _(low=low, n=n):
            cgot[:, low : low + n] = jnp.zeros((gy_n, n) + cgot.shape[2:], F32)

    exchange(moves2, cmine, cgot, s2, r2)()

    for zp in (0, 1):
        for yp in (0, 1):
            at = (zp * 2 + yp) * yc
            for g in range(gy_n):
                f1[zp, yp, :, g * yc : (g + 1) * yc, :] = cgot[g, :, at : at + yc, :]

    c0, c_count = gz * zc, gz_n * zc
    run1(v1, f1, c0, c_count, 0, 0, EVENS, PHASE_A, 0)
    run1(v1, f1, c0, c_count, 1, 0, ODDS, PHASE_B, 1)
    run1(v1, f1, c0, c_count, 0, 1, EVENS - 1, PHASE_C, 2)

    f2 = []
    for i in range(1, EVENS - 1):
        s = [v1e[yp, pl.ds(i, 1)] + v1o[yp, pl.ds(i - 1, 1)] + v1o[yp, pl.ds(i, 1)] for yp in (0, 1)]
        tall = s[0] + pair_sum(s[1], 0, 1)
        f2.append(f1[0, 0, pl.ds(i, 1)] - (27.0 * v1e[0, pl.ds(i, 1)] - (tall + both_sides(tall, 2, 1))))
    q0, q_count = gz * (zc // 2), gz_n * (zc // 2)
    f2e, f2o = f2[0::2], f2[1::2]
    scale2 = [scale_rows(f2[0].shape, q0 - LOW2 + i, q_count) for i in range(7)]
    even2 = [phase2(None, f2e[k], scale2[2 * k], PHASE_A) for k in range(4)]
    odd2 = [phase2(None, f2o[k] + box2(even2[k] + even2[k + 1]), scale2[2 * k + 1], PHASE_B) for k in range(3)]
    for k in (1, 2):
        even2[k] = phase2(even2[k], f2e[k] + box2(odd2[k - 1] + odd2[k]), scale2[2 * k], PHASE_C)
    v2 = [odd2[0], even2[1], odd2[1], even2[2], odd2[2]]
    in_lane = lax.broadcasted_iota(jnp.int32, v2[0].shape, 2) % 2 == 0
    for k in range(5):
        v1e[0, pl.ds(2 + k, 1)] = v1e[0, pl.ds(2 + k, 1)] + jnp.where(in_lane, v2[k], 0.0)

    run1(v1, f1, c0, c_count, 0, 2, 7, PHASE_A, 2)
    run1(v1, f1, c0, c_count, 1, 2, 6, PHASE_B, 2)
    run1(v1, f1, c0, c_count, 0, 3, 6, PHASE_C, 2)

    half = v1e.shape[2]
    for c in range(-1, 6):
        odd = c % 2
        i = (c + LOW1 - odd) // 2
        for yp in (0, 1):
            vc[c + 1, pl.ds(yp, half, stride=2), :] = v1[odd][yp, i]
    ve[0, 0, pl.ds(1, 7)] = ve[0, 0, pl.ds(1, 7)] + vc[...]

    run0(v, f, z0, z_count, 0, 1, 8, PHASE_A, 2)
    run0(v, f, z0, z_count, 1, 1, 7, PHASE_B, 2)
    run0(v, f, z0, z_count, 0, 2, 7, PHASE_C, 2)

    numer = denom = None
    for odd in (0, 1):
        for k in range(zc):
            i = own + k
            here, below, above = pl.ds(i, 1), pl.ds(i - 1 + odd, 1), pl.ds(i + odd, 1)
            p = [[v[odd][yp, xp, here] for xp in (0, 1)] for yp in (0, 1)]
            s = [[p[yp][xp] + v[1 - odd][yp, xp, below] + v[1 - odd][yp, xp, above] for xp in (0, 1)] for yp in (0, 1)]
            b = box0(s)
            for yp, xp in YX:
                image = 27.0 * p[yp][xp] - b[yp][xp]
                numer = add(numer, f[odd][yp, xp, here] * p[yp][xp])
                denom = add(denom, p[yp][xp] * image)
                parity_at = k * 2 + odd
                nat[yp, xp, pl.ds(parity_at, 1)] = image
    rows = numer.shape[1]
    for j, total in enumerate((numer, denom)):
        acc = None
        for r in range(0, rows, 8):
            acc = add(acc, total[0, r : r + 8, :])
        part[j] = acc

    sends, receives = [], []
    for d in range(1, gz_n):
        to = lax.rem(gz + d, gz_n)
        sends.append(pltpu.make_async_remote_copy(
            src_ref=part, dst_ref=parts.at[gz], send_sem=s3.at[d], recv_sem=r3.at[gz],
            device_id=(to, gy), device_id_type=MESH,
        ))
        receives.append(pltpu.make_async_remote_copy(
            src_ref=part, dst_ref=parts.at[to], send_sem=s3.at[d], recv_sem=r3.at[to],
            device_id=(to, gy), device_id_type=MESH,
        ))
    for c in sends:
        c.start()
    parts[gz] = part[...]

    back = permutation(nx, True)
    for which, out in ((0, sol_ref), (1, res_ref)):
        for z in range(zl):
            for yp, xp in YX:
                if which == 0:
                    row = v[z % 2][yp, xp, own + z // 2, pl.ds(gy * y2, y2), :]
                else:
                    row = nat[yp, xp, z, pl.ds(gy * y2, y2), :]
                flat[xp, pl.ds(z * yl + yp, y2, stride=2), :] = row
        out[...] = jnp.dot(
            jnp.concatenate([flat[0], flat[1]], axis=1), back, precision=lax.Precision.HIGHEST, preferred_element_type=F32
        ).reshape(zl, yl, nx)

    for c in receives:
        c.wait_recv()
    for c in sends:
        c.wait_send()
    sums = parts[0]
    for d in range(1, gz_n):
        sums = sums + parts[d]
    alpha = jnp.sum(sums[0], keepdims=True) / jnp.sum(sums[1], keepdims=True)
    alpha = alpha.reshape(1, 1, 1)
    sol_ref[...] = sol_ref[...] * alpha
    res_ref[...] = rhs_ref[...] - res_ref[...] * alpha


def solution(mesh):
    gz_n, gy_n = mesh.shape["gz"], mesh.shape["gy"]

    def body(rhs):
        zl, yl, nx = rhs.shape
        y2, x2 = yl // 2, nx // 2
        y_half = gy_n * y2
        zc, yc = zl // 2, y2 // 2
        vmem = lambda *shape: pltpu.VMEM(shape, F32)
        dma = lambda *shape: pltpu.SemaphoreType.DMA(shape)
        return pl.pallas_call(
            functools.partial(kernel, gz_n, gy_n),
            out_shape=[jax.ShapeDtypeStruct(rhs.shape, F32)] * 2,
            in_specs=[pl.BlockSpec(memory_space=pltpu.VMEM)],
            out_specs=[pl.BlockSpec(memory_space=pltpu.VMEM)] * 2,
            scratch_shapes=[
                vmem(2, zl * yl, x2),
                vmem(zl, 4 * y2, x2),
                vmem(gy_n, WINDOW, 4 * y2, x2),
                vmem(2, 2, EVENS, y_half, x2),
                vmem(2, 2, ODDS, y_half, x2),
                vmem(2, 2, EVENS, y_half, x2),
                vmem(2, 2, ODDS, y_half, x2),
                vmem(zc, y_half, x2),
                vmem(zc // 2, 4 * yc, x2),
                vmem(gy_n, 9, 4 * yc, x2),
                vmem(2, 2, 9, gy_n * yc, x2),
                vmem(2, EVENS, gy_n * yc, x2),
                vmem(2, ODDS, gy_n * yc, x2),
                vmem(7, y_half, x2),
                vmem(2, 8, x2),
                vmem(gz_n, 2, 8, x2),
                vmem(2, 2, zl, y_half, x2),
                dma(3, gy_n), dma(3, gy_n), dma(5, gy_n), dma(5, gy_n), dma(gz_n), dma(gz_n),
            ],
            compiler_params=pltpu.CompilerParams(has_side_effects=True),
        )(rhs)

    return jax.shard_map(
        lambda rhs: tuple(body(rhs)),
        mesh=mesh,
        in_specs=(P("gz", "gy", None),),
        out_specs=(P("gz", "gy", None), P("gz", "gy", None)),
        check_vma=False,
    )
```

time: 504 us -> 37 us (0.07)
  the two profiles are of different devices: /device:TPU:12 before, /device:TPU:0 now
where the time goes in v1:
time: 37 us; the launch traced here: 36.8 us
  Pallas kernels  34 us (92%)
  local copies, waits for them, and re-layouts  2.14 us (6%)
  between operations  0.65 us (2%)
    pallas_call x1, Pallas kernels, body(): pl.pallas_call(functools.partial(kernel, gz_n, gy_n), out_shape=[jax.Shap...  34 us
    unnamed x4, local copies, waits for them, and re-layouts  2.14 us

profile of v1, /device:TPU:0, one launch (start us, length us, event | category | flops | bytes accessed | tf_op | source)
XLA Modules:
  0.0 36.8 jit_solution(3355136527564349860)
XLA Ops:
  0.6 34.0 %shard_map.30 = (f32[8,8,256]{2,1,0:T(8,128)}, f32[8,8,256]{2,1,0:T(8,128)}) custom-call(f32[8,8,256]{2,1,0:T(8,128)} %rhs_ref.1), custom_call_target="tpu_custom_call" | custom-call | tf_op jit(solution)/shard_map/pallas_call | solution.py:387
  34.6 0.0 copy-start
  34.6 1.5 %copy.5 = f32[8,8,256]{2,1,0:T(8,128)} copy(f32[8,8,256]{2,1,0:T(8,128)} %get-tuple-element.4) | data formatting | bytes 131072
  36.1 0.0 copy-done
  36.1 0.6 %copy.6 = f32[8,8,256]{2,1,0:T(8,128)} copy(f32[8,8,256]{2,1,0:T(8,128)S(1)} %copy-done) | data formatting | bytes 131072
Async XLA Ops:
  34.6 1.5 %copy-start = (f32[8,8,256]{2,1,0:T(8,128)S(1)}, f32[8,8,256]{2,1,0:T(8,128)}, u32[]{:S(2)}) copy-start(f32[8,8,256]{2,1,0:T(8,128)} %get-tuple-element.5) | copy-start | bytes 196612

commit v2 on v1

--- a/solution.py
+++ b/solution.py
@@ -156,7 +156,7 @@
 def kernel(
     gz_n, gy_n, rhs_ref, sol_ref, res_ref,
     flat, mine, got, fe, fo, ve, vo, dbuf, cmine, cgot, f1, v1e, v1o, vc, part, parts, nat,
-    s1, r1, s2, r2, s3, r3,
+    s1, r1, s2, r2, s3, r3, s4,
 ):
     gz, gy = lax.axis_index("gz"), lax.axis_index("gy")
     zl, yl, nx = rhs_ref.shape
@@ -170,6 +170,21 @@
 
     def there(dz):
         return (gz + dz >= 0) & (gz + dz < gz_n)
+
+    barrier = pltpu.get_barrier_semaphore()
+    count = jnp.int32(0)
+    for dz in range(1 - gz_n, gz_n):
+        for dg in range(gy_n if abs(dz) <= 2 else 1):
+            if dz == 0 and dg == 0:
+                continue
+
+            @pl.when(there(dz))
+            def _(dz=dz, dg=dg):
+                pl.semaphore_signal(
+                    barrier, inc=1, device_id=(gz + dz, lax.rem(gy + dg, gy_n)), device_id_type=MESH
+                )
+
+            count = count + there(dz).astype(jnp.int32)
 
     split = jnp.dot(
         rhs_ref[...].reshape(zl * yl, nx), permutation(nx, False),
@@ -196,6 +211,71 @@
     moves2 = {
         -2: (0, zc // 2, 7), -1: (0, zc // 2, 5), 0: (0, zc // 2, 3), 1: (0, zc // 2, 1), 2: (zc // 2 - 1, 1, 0),
     }
+
+    order1 = [
+        (slot, dz, h) for h in range(gy_n // 2) for slot, dz in ((2, 0), (0, 1), (1, -1)) if dz != 0 or h != 0
+    ]
+
+    def gather():
+        sibling = gy + 1 - 2 * lax.rem(gy, 2)
+
+        def blocks(act):
+            for slot, dz in enumerate((1, -1, 0)):
+                for h in range(gy_n // 2):
+                    if dz == 0 and h == 0:
+                        continue
+                    act(slot, dz, h)
+
+        def when_there(dz, go):
+            if dz == 0:
+                go()
+            else:
+                pl.when(there(dz))(go)
+
+        def direct(slot, dz, h, owner):
+            first, n, to = moves1[dz]
+            g = lax.rem(gy + 2 * h, gy_n)
+            return pltpu.make_async_remote_copy(
+                src_ref=mine.at[pl.ds(first, n)],
+                dst_ref=got.at[g if owner else gy, pl.ds(to, n)],
+                send_sem=s1.at[slot, h],
+                recv_sem=r1.at[slot, g if owner else gy],
+                device_id=(gz - dz if owner else gz + dz, g),
+                device_id_type=MESH,
+            )
+
+        def relay(slot, dz, h, owner):
+            _, n, to = moves1[dz]
+            g = lax.rem((sibling if owner else gy) + 2 * h, gy_n)
+            place = got.at[g, pl.ds(to, n)]
+            return pltpu.make_async_remote_copy(
+                src_ref=mine if dz == 0 and h == 0 else place,
+                dst_ref=place,
+                send_sem=s4.at[slot, h],
+                recv_sem=r1.at[slot, g],
+                device_id=(gz, sibling),
+                device_id_type=MESH,
+            )
+
+        blocks(lambda slot, dz, h: when_there(dz, lambda: direct(slot, dz, h, False).start()))
+        relay(2, 0, 0, False).start()
+
+        def forward(slot, dz, h):
+            def go():
+                direct(slot, dz, h, True).wait_recv()
+                relay(slot, dz, h, False).start()
+
+            when_there(-dz, go)
+
+        for slot, dz, h in order1:
+            forward(slot, dz, h)
+        relay(2, 0, 0, True).wait_recv()
+        for slot, dz, h in order1:
+            when_there(-dz, lambda: relay(slot, dz, h, True).wait_recv())
+        relay(2, 0, 0, False).wait_send()
+        for slot, dz, h in order1:
+            when_there(-dz, lambda: relay(slot, dz, h, False).wait_send())
+        blocks(lambda slot, dz, h: when_there(dz, lambda: direct(slot, dz, h, False).wait_send()))
 
     def exchange(moves, source, target, ssem, rsem):
         sends, receives = [], []
@@ -239,7 +319,8 @@
         each(sends, lambda c: c.start())
         return lambda: (each(receives, lambda c: c.wait_recv()), each(sends, lambda c: c.wait_send()))
 
-    exchange(moves1, mine, got, s1, r1)()
+    pl.semaphore_wait(barrier, count)
+    gather()
 
     for q in range(WINDOW):
         for k, (yp, xp) in enumerate(YX):
@@ -331,7 +412,7 @@
         acc = None
         for r in range(0, rows, 8):
             acc = add(acc, total[0, r : r + 8, :])
-        part[j] = acc
+        part[pl.ds(j, 1), :] = jnp.sum(acc, axis=0, keepdims=True)
 
     sends, receives = [], []
     for d in range(1, gz_n):
@@ -368,7 +449,7 @@
     sums = parts[0]
     for d in range(1, gz_n):
         sums = sums + parts[d]
-    alpha = jnp.sum(sums[0], keepdims=True) / jnp.sum(sums[1], keepdims=True)
+    alpha = jnp.sum(sums[0:1], axis=1, keepdims=True) / jnp.sum(sums[1:2], axis=1, keepdims=True)
     alpha = alpha.reshape(1, 1, 1)
     sol_ref[...] = sol_ref[...] * alpha
     res_ref[...] = rhs_ref[...] - res_ref[...] * alpha
@@ -404,12 +485,12 @@
                 vmem(2, EVENS, gy_n * yc, x2),
                 vmem(2, ODDS, gy_n * yc, x2),
                 vmem(7, y_half, x2),
-                vmem(2, 8, x2),
-                vmem(gz_n, 2, 8, x2),
+                vmem(2, x2),
+                vmem(gz_n, 2, x2),
                 vmem(2, 2, zl, y_half, x2),
-                dma(3, gy_n), dma(3, gy_n), dma(5, gy_n), dma(5, gy_n), dma(gz_n), dma(gz_n),
+                dma(3, gy_n), dma(3, gy_n), dma(5, gy_n), dma(5, gy_n), dma(gz_n), dma(gz_n), dma(3, gy_n),
             ],
-            compiler_params=pltpu.CompilerParams(has_side_effects=True),
+            compiler_params=pltpu.CompilerParams(has_side_effects=True, collective_id=0),
         )(rhs)
 
     return jax.shard_map(

time: 37 us -> 30.5 us (0.82)
  Pallas kernels: 34 us -> 27.5 us
    pallas_call x1, Pallas kernels: 34 us -> 27.5 us  [body(): pl.pallas_call(functools.partial(kernel, gz_n, gy_n), out_shape=[jax.Shap...]
where the time goes in v2:
time: 30.5 us; the launch traced here: 30.2 us
  Pallas kernels  27.5 us (90%)
  local copies, waits for them, and re-layouts  2.14 us (7%)
  between operations  0.65 us (2%)
    pallas_call x1, Pallas kernels, body(): pl.pallas_call(functools.partial(kernel, gz_n, gy_n), out_shape=[jax.Shap...  27.5 us
    unnamed x4, local copies, waits for them, and re-layouts  2.14 us

profile of v2, /device:TPU:0, one launch (start us, length us, event | category | flops | bytes accessed | tf_op | source)
XLA Modules:
  0.0 30.2 jit_solution(17869905517815171663)
XLA Ops:
  0.6 27.5 %shard_map.30 = (f32[8,8,256]{2,1,0:T(8,128)}, f32[8,8,256]{2,1,0:T(8,128)}) custom-call(f32[8,8,256]{2,1,0:T(8,128)} %rhs_ref.1), custom_call_target="tpu_custom_call" | custom-call | tf_op jit(solution)/shard_map/pallas_call | solution.py:468
  28.1 0.0 copy-start
  28.1 1.5 %copy.5 = f32[8,8,256]{2,1,0:T(8,128)} copy(f32[8,8,256]{2,1,0:T(8,128)} %get-tuple-element.4) | data formatting | bytes 131072
  29.6 0.0 copy-done
  29.6 0.6 %copy.6 = f32[8,8,256]{2,1,0:T(8,128)} copy(f32[8,8,256]{2,1,0:T(8,128)S(1)} %copy-done) | data formatting | bytes 131072
Async XLA Ops:
  28.1 1.5 %copy-start = (f32[8,8,256]{2,1,0:T(8,128)S(1)}, f32[8,8,256]{2,1,0:T(8,128)}, u32[]{:S(2)}) copy-start(f32[8,8,256]{2,1,0:T(8,128)} %get-tuple-element.5) | copy-start | bytes 196612

commit v3 on v2

--- a/solution.py
+++ b/solution.py
@@ -154,12 +154,14 @@
 
 
 def kernel(
-    gz_n, gy_n, rhs_ref, sol_ref, res_ref,
+    gz_n, gy_n, rhs_hbm, sol_ref, res_ref,
     flat, mine, got, fe, fo, ve, vo, dbuf, cmine, cgot, f1, v1e, v1o, vc, part, parts, nat,
-    s1, r1, s2, r2, s3, r3, s4,
+    s1, r1, s2, r2, s3, r3, s4, rhs_ref, s5,
 ):
     gz, gy = lax.axis_index("gz"), lax.axis_index("gy")
     zl, yl, nx = rhs_ref.shape
+    fetch = pltpu.make_async_copy(rhs_hbm, rhs_ref, s5)
+    fetch.start()
     y2, x2 = yl // 2, nx // 2
     yc = y2 // 2
     zc = zl // 2
@@ -186,6 +188,7 @@
 
             count = count + there(dz).astype(jnp.int32)
 
+    fetch.wait()
     split = jnp.dot(
         rhs_ref[...].reshape(zl * yl, nx), permutation(nx, False),
         precision=lax.Precision.HIGHEST, preferred_element_type=F32,
@@ -468,7 +471,7 @@
         return pl.pallas_call(
             functools.partial(kernel, gz_n, gy_n),
             out_shape=[jax.ShapeDtypeStruct(rhs.shape, F32)] * 2,
-            in_specs=[pl.BlockSpec(memory_space=pltpu.VMEM)],
+            in_specs=[pl.BlockSpec(memory_space=pl.ANY)],
             out_specs=[pl.BlockSpec(memory_space=pltpu.VMEM)] * 2,
             scratch_shapes=[
                 vmem(2, zl * yl, x2),
@@ -489,6 +492,7 @@
                 vmem(gz_n, 2, x2),
                 vmem(2, 2, zl, y_half, x2),
                 dma(3, gy_n), dma(3, gy_n), dma(5, gy_n), dma(5, gy_n), dma(gz_n), dma(gz_n), dma(3, gy_n),
+                vmem(zl, yl, nx), pltpu.SemaphoreType.DMA,
             ],
             compiler_params=pltpu.CompilerParams(has_side_effects=True, collective_id=0),
         )(rhs)

time: 30.5 us -> 29.8 us (0.977)
  Pallas kernels: 27.5 us -> 26.8 us
    pallas_call x1, Pallas kernels: 27.5 us -> 26.8 us  [body(): pl.pallas_call(functools.partial(kernel, gz_n, gy_n), out_shape=[jax.Shap...]
where the time goes in v3:
time: 29.8 us; the launch traced here: 29.6 us
  Pallas kernels  26.8 us (90%)
  local copies, waits for them, and re-layouts  2.14 us (7%)
  between operations  0.65 us (2%)
    pallas_call x1, Pallas kernels, body(): pl.pallas_call(functools.partial(kernel, gz_n, gy_n), out_shape=[jax.Shap...  26.8 us
    unnamed x4, local copies, waits for them, and re-layouts  2.14 us

profile of v3, /device:TPU:0, one launch (start us, length us, event | category | flops | bytes accessed | tf_op | source)
XLA Modules:
  0.0 29.6 jit_solution(2518370971391067673)
XLA Ops:
  0.6 26.8 %shard_map.30 = (f32[8,8,256]{2,1,0:T(8,128)}, f32[8,8,256]{2,1,0:T(8,128)}) custom-call(f32[8,8,256]{2,1,0:T(8,128)} %rhs_hbm.1), custom_call_target="tpu_custom_call" | custom-call | tf_op jit(solution)/shard_map/pallas_call | solution.py:471
  27.5 0.0 copy-start
  27.5 1.5 %copy.5 = f32[8,8,256]{2,1,0:T(8,128)} copy(f32[8,8,256]{2,1,0:T(8,128)} %get-tuple-element.4) | data formatting | bytes 131072
  29.0 0.0 copy-done
  29.0 0.6 %copy.6 = f32[8,8,256]{2,1,0:T(8,128)} copy(f32[8,8,256]{2,1,0:T(8,128)S(1)} %copy-done) | data formatting | bytes 131072
Async XLA Ops:
  27.5 1.5 %copy-start = (f32[8,8,256]{2,1,0:T(8,128)S(1)}, f32[8,8,256]{2,1,0:T(8,128)}, u32[]{:S(2)}) copy-start(f32[8,8,256]{2,1,0:T(8,128)} %get-tuple-element.5) | copy-start | bytes 196612
